TPU v7x, 32 devices: a whole 2x2x4 slice. The times are simulated.
32 devices in a mesh: site: 2 (over core), replica: 4 (over z), model: 4 (over y, x).
Axes of the slice: x: 2, y: 2, z: 4, core: 2. Of those that a mesh axis runs over, the one named last changes fastest.
Arguments:
- partial_query: bfloat16 [8, 1024, 1024], P(('site', 'replica'), None, 'model'), parts along dimension 0, may hold values from -4 to 4
- partial_key: bfloat16 [8, 1024, 1024], P(('site', 'replica'), None, 'model'), parts along dimension 0, may hold values from -4 to 4
- partial_value: bfloat16 [8, 1024, 1024], P(('site', 'replica'), None, 'model'), parts along dimension 0, may hold values from -4 to 4
- partial_mixed: bfloat16 [8, 1024, 1024], P(('site', 'replica'), 'model'), parts along dimension 0, may hold values from -4 to 4
- partial_norm: bfloat16 [8, 1024], P(('site', 'replica')), parts along dimension 0, may hold values from -8 to 8
- master_query: float32 [2048, 1024], P(('site', 'replica'), 'model'), parts along dimension 0, may hold values from -0.1875 to 0.1875
- master_key: float32 [2048, 1024], P(('site', 'replica'), 'model'), parts along dimension 0, may hold values from -0.1875 to 0.1875
- master_value: float32 [2048, 1024], P(('site', 'replica'), 'model'), parts along dimension 0, may hold values from -0.1875 to 0.1875
- master_mixed: float32 [2048, 1024], P(('site', 'model'), 'replica'), parts along dimension 0, may hold values from -0.1875 to 0.1875
- master_norm: float32 [2048], P(('site', 'replica')), parts along dimension 0, may hold values from 0.25 to 1.75
- memory_query: float32 [2048, 1024], P(('site', 'replica'), 'model'), parts along dimension 0, may hold values from 0.05 to 0.8
- memory_key: float32 [2048, 1024], P(('site', 'replica'), 'model'), parts along dimension 0, may hold values from 0.05 to 0.8
- memory_value: float32 [2048, 1024], P(('site', 'replica'), 'model'), parts along dimension 0, may hold values from 0.05 to 0.8
- memory_mixed: float32 [2048, 1024], P(('site', 'model'), 'replica'), parts along dimension 0, may hold values from 0.05 to 0.8
- memory_norm: float32 [2048], P(('site', 'replica')), parts along dimension 0, may hold values from 0.05 to 0.8
Outputs:
- compute_query: bfloat16 [2048, 1024], P('site', 'model'), parts along dimension 0
- compute_key: bfloat16 [2048, 1024], P('site', 'model'), parts along dimension 0
- compute_value: bfloat16 [2048, 1024], P('site', 'model'), parts along dimension 0
- compute_mixed: bfloat16 [2048, 1024], P(('site', 'model')), parts along dimension 0
- compute_norm: bfloat16 [2048], P('site'), parts along dimension 0
- stepped_query: float32 [2048, 1024], P(('site', 'replica'), 'model'), parts along dimension 0
- stepped_key: float32 [2048, 1024], P(('site', 'replica'), 'model'), parts along dimension 0
- stepped_value: float32 [2048, 1024], P(('site', 'replica'), 'model'), parts along dimension 0
- stepped_mixed: float32 [2048, 1024], P(('site', 'model'), 'replica'), parts along dimension 0
- stepped_norm: float32 [2048], P(('site', 'replica')), parts along dimension 0
- state_new_query: float32 [2048, 1024], P(('site', 'replica'), 'model'), parts along dimension 0
- state_new_key: float32 [2048, 1024], P(('site', 'replica'), 'model'), parts along dimension 0
- state_new_value: float32 [2048, 1024], P(('site', 'replica'), 'model'), parts along dimension 0
- state_new_mixed: float32 [2048, 1024], P(('site', 'model'), 'replica'), parts along dimension 0
- state_new_norm: float32 [2048], P(('site', 'replica')), parts along dimension 0
There are 2 independent parts, one for each index of `site`. A program takes and returns all parts, laid end to end along the dimension named above; each array names one. Nothing has to cross between parts.
All inputs are finite; a program needn't handle non-finite values.
Results may differ from a plain program's by a relative error of at most 0.001.
Values may be sent and summed in bfloat16 or wider, within the bound.
No kernel may reach another device: no remote copies, remote signals or barrier semaphores. Data moves between devices by JAX's collectives and lax.ppermute only.
A program may use at most 64 MiB of HBM per device.

v0:
```python
import jax
import jax.numpy as jnp
from jax import lax
from jax.sharding import PartitionSpec as P

learn_rate = 0.05
hold_rate = 0.7


def body(
    partial_query,
    partial_key,
    partial_value,
    partial_mixed,
    partial_norm,
    master_query,
    master_key,
    master_value,
    master_mixed,
    master_norm,
    memory_query,
    memory_key,
    memory_value,
    memory_mixed,
    memory_norm,
):
    mean_query, mean_key, mean_value, mean_mixed = (
        lax.psum_scatter(
            partial_query[0].astype(jnp.float32), "replica", scatter_dimension=0, tiled=True
        ),
        lax.psum_scatter(
            partial_key[0].astype(jnp.float32), "replica", scatter_dimension=0, tiled=True
        ),
        lax.psum_scatter(
            partial_value[0].astype(jnp.float32), "replica", scatter_dimension=0, tiled=True
        ),
        lax.psum_scatter(
            partial_mixed[0].astype(jnp.float32), "replica", scatter_dimension=1, tiled=True
        ),
    )
    whole_norm = lax.psum(partial_norm[0].astype(jnp.float32), "replica")
    place = lax.axis_index("replica")
    mean_norm = lax.dynamic_slice_in_dim(
        whole_norm, place * master_norm.shape[0], master_norm.shape[0]
    )
    mean_rate = lax.axis_size("replica") ** (-0.5)
    mean_query = mean_query * mean_rate
    mean_key = mean_key * mean_rate
    mean_value = mean_value * mean_rate
    mean_mixed = mean_mixed * mean_rate
    mean_norm = mean_norm * mean_rate
    state_new_query = hold_rate * memory_query + (1.0 - hold_rate) * mean_query * mean_query
    stepped_query = master_query - learn_rate * mean_query * lax.rsqrt(state_new_query + 1e-06)
    state_new_key = hold_rate * memory_key + (1.0 - hold_rate) * mean_key * mean_key
    stepped_key = master_key - learn_rate * mean_key * lax.rsqrt(state_new_key + 1e-06)
    state_new_value = hold_rate * memory_value + (1.0 - hold_rate) * mean_value * mean_value
    stepped_value = master_value - learn_rate * mean_value * lax.rsqrt(state_new_value + 1e-06)
    state_new_mixed = hold_rate * memory_mixed + (1.0 - hold_rate) * mean_mixed * mean_mixed
    stepped_mixed = master_mixed - learn_rate * mean_mixed * lax.rsqrt(state_new_mixed + 1e-06)
    state_new_norm = hold_rate * memory_norm + (1.0 - hold_rate) * mean_norm * mean_norm
    stepped_norm = master_norm - learn_rate * mean_norm * lax.rsqrt(state_new_norm + 1e-06)
    compute_query, compute_key, compute_value, compute_mixed, compute_norm = (
        lax.all_gather(stepped_query.astype(jnp.bfloat16), "replica", axis=0, tiled=True),
        lax.all_gather(stepped_key.astype(jnp.bfloat16), "replica", axis=0, tiled=True),
        lax.all_gather(stepped_value.astype(jnp.bfloat16), "replica", axis=0, tiled=True),
        lax.all_gather(stepped_mixed.astype(jnp.bfloat16), "replica", axis=1, tiled=True),
        lax.all_gather(stepped_norm.astype(jnp.bfloat16), "replica", axis=0, tiled=True),
    )
    return (
        compute_query,
        compute_key,
        compute_value,
        compute_mixed,
        compute_norm,
        stepped_query,
        stepped_key,
        stepped_value,
        stepped_mixed,
        stepped_norm,
        state_new_query,
        state_new_key,
        state_new_value,
        state_new_mixed,
        state_new_norm,
    )


def solution(mesh):
    placed = (
        P(("site", "replica"), None, "model"),
        P(("site", "replica"), None, "model"),
        P(("site", "replica"), None, "model"),
        P(("site", "replica"), "model", None),
        P(("site", "replica"), None),
        P(("site", "replica"), "model"),
        P(("site", "replica"), "model"),
        P(("site", "replica"), "model"),
        P(("site", "model"), "replica"),
        P(("site", "replica")),
        P(("site", "replica"), "model"),
        P(("site", "replica"), "model"),
        P(("site", "replica"), "model"),
        P(("site", "model"), "replica"),
        P(("site", "replica")),
    )
    return jax.shard_map(
        body,
        mesh=mesh,
        in_specs=placed,
        out_specs=(
            P("site", "model"),
            P("site", "model"),
            P("site", "model"),
            P(("site", "model"), None),
            P("site"),
            P(("site", "replica"), "model"),
            P(("site", "replica"), "model"),
            P(("site", "replica"), "model"),
            P(("site", "model"), "replica"),
            P(("site", "replica")),
            P(("site", "replica"), "model"),
            P(("site", "replica"), "model"),
            P(("site", "replica"), "model"),
            P(("site", "model"), "replica"),
            P(("site", "replica")),
        ),
        check_vma=False,
    )
```

profile of v0, /device:TPU:0, one launch (start us, length us, event | category | flops | bytes accessed | tf_op | source)
XLA Modules:
  0.0 167.0 jit_solution(16219474354706718690)
XLA Ops:
  7.2 0.0 reduce-scatter.5.cloned.1.call-start
  7.2 2.1 %bitcast_convert_fusion.3 = f32[1024,256]{1,0:T(8,128)} fusion(bf16[1,1024,256]{2,1,0:T(8,128)(2,1)} %param.15), kind=kLoop, calls=%fused_computation.3 | loop fusion | flops 262144 | bytes 1572864 | tf_op jit(solution)/shard_map/convert_element_type | solution.py:29
  9.3 0.0 copy-start
  9.3 0.0 reduce-scatter.5.cloned.1.call-update
  9.3 0.0 reduce-scatter.7.cloned.1.call-start
  9.4 1.0 copy-done
  10.4 1.1 bitcast_convert_fusion.2
  11.4 0.0 copy-start.1
  11.4 0.0 reduce-scatter.7.cloned.1.call-update
  11.5 0.0 reduce-scatter.9.cloned.1.call-start
  11.5 1.0 copy-done.1
  12.5 1.0 bitcast_convert_fusion.1
  13.5 0.0 copy-start.2
  13.5 0.0 reduce-scatter.9.cloned.1.call-update
  13.5 0.0 reduce-scatter.11.cloned.1.call-start
  13.6 1.0 copy-done.2
  14.6 1.1 bitcast_convert_fusion
  15.7 0.0 copy-start.11
  15.7 0.0 copy-start.3
  15.7 0.0 copy-start.4
  15.7 0.0 reduce-scatter.11.cloned.1.call-update
  15.7 0.7 copy-done.11
  16.4 0.0 copy-start.12
  16.4 0.0 copy-start.13
  16.4 14.0 %psum.7 = f32[1024]{0:T(1024)S(1)} all-reduce(f32[1024]{0:T(1024)S(1)} %bitcast.15), channel_id=1, replica_groups=mesh['site'=2,'replica'=4,'model'=4] {'replica'}, use_global_device_ids=true, to_apply=%region_4.0 | all-reduce | flops 1024 | bytes 8192 | tf_op jit(solution)/shard_map/psum | solution.py:41
  30.3 0.0 copy-done.12
  30.3 0.0 copy-done.13
  30.3 0.7 fusion
  31.0 7.7 %all-gather = bf16[4,1,256]{2,1,0:T(2,128)(2,1)S(1)} all-gather(bf16[1,1,256]{2,1,0:T(2,128)(2,1)S(1)} %reshape.45), channel_id=1, replica_groups=mesh['site'=2,'replica'=4,'model'=4] {'replica'}, dimensions={0}, use_global_device_ids=true | all-gather | bytes 2560 | tf_op jit(solution)/shard_map/all_gather | solution.py:67
  38.8 0.6 copy.30
  39.3 1.3 reduce-scatter.5.cloned.1.call-done
  40.6 0.0 copy-done.3
  40.7 0.0 copy-done.4
  40.7 1.8 %fusion.4 = (bf16[256,256]{1,0:T(8,128)(2,1)S(1)}, f32[256,256]{1,0:T(8,128)}, f32[256,256]{1,0:T(8,128)}) fusion(f32[256,256]{1,0:T(8,128)S(1)} %copy-done.3, f32[256,256]{1,0:T(8,128)} %reduce-scatter.5.cloned.1.call-done, f32[256,256]{1,0:T(8,128)S(1)} %copy-done.4), kind=kLoop, calls=%fused_computation.18 | loop fusion | flops 655360 | bytes 1441792 | tf_op jit(solution)/shard_map/convert_element_type | solution.py:63
  42.5 0.0 copy-start.5
  42.5 0.0 copy-start.6
  42.5 19.5 %all_gather.15 = bf16[1024,256]{1,0:T(8,128)(2,1)S(1)} all-gather(bf16[256,256]{1,0:T(8,128)(2,1)S(1)} %get-tuple-element.27), channel_id=1, replica_groups=mesh['site'=2,'replica'=4,'model'=4] {'replica'}, dimensions={0}, use_global_device_ids=true | all-gather | bytes 655360 | tf_op jit(solution)/shard_map/all_gather | solution.py:63
  62.0 10.9 %reduce-scatter.7.cloned.1.call-done = f32[256,256]{1,0:T(8,128)} async-done(((f32[1024,256]{1,0:T(8,128)}), f32[256,256]{1,0:T(8,128)}) %reduce-scatter.7.cloned.1.call-update) | async-done | bytes 262160 | tf_op jit(solution)/shard_map/reduce_scatter | solution.py:31
  72.9 0.0 copy-done.5
  72.9 0.0 copy-done.6
  72.9 1.8 %fusion.3 = (bf16[256,256]{1,0:T(8,128)(2,1)S(1)}, f32[256,256]{1,0:T(8,128)}, f32[256,256]{1,0:T(8,128)}) fusion(f32[256,256]{1,0:T(8,128)S(1)} %copy-done.5, f32[256,256]{1,0:T(8,128)} %reduce-scatter.7.cloned.1.call-done, f32[256,256]{1,0:T(8,128)S(1)} %copy-done.6), kind=kLoop, calls=%fused_computation.17 | loop fusion | flops 655360 | bytes 1441792 | tf_op jit(solution)/shard_map/convert_element_type | solution.py:64
  74.7 0.0 copy-start.7
  74.7 0.0 copy-start.8
  74.7 19.7 %all_gather.16 = bf16[1024,256]{1,0:T(8,128)(2,1)S(1)} all-gather(bf16[256,256]{1,0:T(8,128)(2,1)S(1)} %get-tuple-element.24), channel_id=1, replica_groups=mesh['site'=2,'replica'=4,'model'=4] {'replica'}, dimensions={0}, use_global_device_ids=true | all-gather | bytes 655360 | tf_op jit(solution)/shard_map/all_gather | solution.py:64
  94.4 12.1 %reduce-scatter.9.cloned.1.call-done = f32[256,256]{1,0:T(8,128)} async-done(((f32[1024,256]{1,0:T(8,128)}), f32[256,256]{1,0:T(8,128)}) %reduce-scatter.9.cloned.1.call-update) | async-done | bytes 262160 | tf_op jit(solution)/shard_map/reduce_scatter | solution.py:34
  106.5 0.0 copy-done.7
  106.5 0.0 copy-done.8
  106.5 1.8 %fusion.2 = (bf16[256,256]{1,0:T(8,128)(2,1)S(1)}, f32[256,256]{1,0:T(8,128)}, f32[256,256]{1,0:T(8,128)}) fusion(f32[256,256]{1,0:T(8,128)S(1)} %copy-done.7, f32[256,256]{1,0:T(8,128)} %reduce-scatter.9.cloned.1.call-done, f32[256,256]{1,0:T(8,128)S(1)} %copy-done.8), kind=kLoop, calls=%fused_computation.16 | loop fusion | flops 655360 | bytes 1441792 | tf_op jit(solution)/shard_map/convert_element_type | solution.py:65
  108.4 0.0 copy-start.9
  108.4 0.0 copy-start.10
  108.4 19.6 %all_gather.17 = bf16[1024,256]{1,0:T(8,128)(2,1)S(1)} all-gather(bf16[256,256]{1,0:T(8,128)(2,1)S(1)} %get-tuple-element.21), channel_id=1, replica_groups=mesh['site'=2,'replica'=4,'model'=4] {'replica'}, dimensions={0}, use_global_device_ids=true | all-gather | bytes 655360 | tf_op jit(solution)/shard_map/all_gather | solution.py:65
  128.0 11.8 %reduce-scatter.11.cloned.1.call-done = f32[256,256]{1,0:T(8,128)} async-done(((f32[256,1024]{1,0:T(8,128)}), f32[256,256]{1,0:T(8,128)}) %reduce-scatter.11.cloned.1.call-update) | async-done | bytes 262160 | tf_op jit(solution)/shard_map/reduce_scatter | solution.py:37
  139.8 0.0 copy-done.9
  139.8 0.0 copy-done.10
  139.8 1.8 %fusion.1 = (bf16[256,256]{1,0:T(8,128)(2,1)S(1)}, f32[256,256]{1,0:T(8,128)}, f32[256,256]{1,0:T(8,128)}) fusion(f32[256,256]{1,0:T(8,128)S(1)} %copy-done.9, f32[256,256]{1,0:T(8,128)} %reduce-scatter.11.cloned.1.call-done, f32[256,256]{1,0:T(8,128)S(1)} %copy-done.10), kind=kLoop, calls=%fused_computation.15 | loop fusion | flops 655360 | bytes 1441792 | tf_op jit(solution)/shard_map/convert_element_type | solution.py:66
  141.6 15.7 %all_gather.18 = bf16[256,1024]{1,0:T(8,128)(2,1)S(1)} all-gather(bf16[256,256]{1,0:T(8,128)(2,1)S(1)} %get-tuple-element.18), channel_id=1, replica_groups=mesh['site'=2,'replica'=4,'model'=4] {'replica'}, dimensions={1}, use_global_device_ids=true | all-gather | bytes 655360 | tf_op jit(solution)/shard_map/all_gather | solution.py:66
  157.3 0.8 copy.35
  158.1 0.8 copy.36
  158.9 0.8 copy.37
  159.7 0.8 copy.38
  (3 shorter events, 0.0 us)
Async XLA Ops:
  7.2 33.5 %reduce-scatter.5.cloned.1.call-start = ((), (), s32[]{:S(2)}) async-start(), calls=%async_computation.4 | async-start | bytes 1310720 | tf_op jit(solution)/shard_map/reduce_scatter | solution.py:28
  9.3 1.0 copy-start
  9.3 63.6 %reduce-scatter.7.cloned.1.call-start = ((), (), s32[]{:S(2)}) async-start(), calls=%async_computation.5 | async-start | bytes 1310720 | tf_op jit(solution)/shard_map/reduce_scatter | solution.py:31
  11.4 1.0 copy-start.1
  11.5 95.1 %reduce-scatter.9.cloned.1.call-start = ((), (), s32[]{:S(2)}) async-start(), calls=%async_computation.6 | async-start | bytes 1310720 | tf_op jit(solution)/shard_map/reduce_scatter | solution.py:34
  13.5 1.0 copy-start.2
  13.5 126.2 %reduce-scatter.11.cloned.1.call-start = ((), (), s32[]{:S(2)}) async-start(), calls=%async_computation.7 | async-start | bytes 1310720 | tf_op jit(solution)/shard_map/reduce_scatter | solution.py:37
  15.7 0.7 copy-start.11
  15.7 25.0 %copy-start.3 = (f32[256,256]{1,0:T(8,128)S(1)}, f32[256,256]{1,0:T(8,128)}, u32[]{:S(2)}) copy-start(f32[256,256]{1,0:T(8,128)} %param.20) | copy-start | bytes 786436
  15.7 25.0 %copy-start.4 = (f32[256,256]{1,0:T(8,128)S(1)}, f32[256,256]{1,0:T(8,128)}, u32[]{:S(2)}) copy-start(f32[256,256]{1,0:T(8,128)} %param.25) | copy-start | bytes 786436
  16.4 14.0 %copy-start.12 = (f32[256]{0:T(256)S(1)}, f32[256]{0:T(256)}, u32[]{:S(2)}) copy-start(f32[256]{0:T(256)} %param.24) | copy-start | bytes 3076
  16.4 14.0 %copy-start.13 = (f32[256]{0:T(256)S(1)}, f32[256]{0:T(256)}, u32[]{:S(2)}) copy-start(f32[256]{0:T(256)} %param.29) | copy-start | bytes 3076
  42.5 30.4 %copy-start.5 = (f32[256,256]{1,0:T(8,128)S(1)}, f32[256,256]{1,0:T(8,128)}, u32[]{:S(2)}) copy-start(f32[256,256]{1,0:T(8,128)} %param.21) | copy-start | bytes 786436
  42.5 30.4 %copy-start.6 = (f32[256,256]{1,0:T(8,128)S(1)}, f32[256,256]{1,0:T(8,128)}, u32[]{:S(2)}) copy-start(f32[256,256]{1,0:T(8,128)} %param.26) | copy-start | bytes 786436
  74.7 31.8 %copy-start.7 = (f32[256,256]{1,0:T(8,128)S(1)}, f32[256,256]{1,0:T(8,128)}, u32[]{:S(2)}) copy-start(f32[256,256]{1,0:T(8,128)} %param.22) | copy-start | bytes 786436
  74.7 31.8 %copy-start.8 = (f32[256,256]{1,0:T(8,128)S(1)}, f32[256,256]{1,0:T(8,128)}, u32[]{:S(2)}) copy-start(f32[256,256]{1,0:T(8,128)} %param.27) | copy-start | bytes 786436
  108.4 31.4 %copy-start.9 = (f32[256,256]{1,0:T(8,128)S(1)}, f32[256,256]{1,0:T(8,128)}, u32[]{:S(2)}) copy-start(f32[256,256]{1,0:T(8,128)} %param.23) | copy-start | bytes 786436
  108.4 31.4 %copy-start.10 = (f32[256,256]{1,0:T(8,128)S(1)}, f32[256,256]{1,0:T(8,128)}, u32[]{:S(2)}) copy-start(f32[256,256]{1,0:T(8,128)} %param.28) | copy-start | bytes 786436
Sparse Core Ops, SparseCore 0:
  10.3 30.3 reduce-scatter.4
  42.9 29.9 reduce-scatter.6
  75.2 31.2 reduce-scatter.8
  108.7 31.0 reduce-scatter.10
where the time goes:
time: 168 us; the launch traced here: 167 us
  blocking collectives  96.2 us (57%)
  waiting for transfers between devices  36.2 us (22%)
  between operations  13.8 us (8%)
  other arithmetic  13.3 us (8%)
  local copies, waits for them, and re-layouts  7.35 us (4%)
    all_gather x1, blocking collectives, body(): lax.all_gather(stepped_key.astype(jnp.bfloat16), 'replica', axis=0, tiled...  19.7 us
    all_gather x1, blocking collectives, body(): lax.all_gather(stepped_value.astype(jnp.bfloat16), 'replica', axis=0, til...  19.6 us
    all_gather x1, blocking collectives, body(): lax.all_gather(stepped_query.astype(jnp.bfloat16), 'replica', axis=0, til...  19.5 us
    all_gather x1, blocking collectives, body(): lax.all_gather(stepped_mixed.astype(jnp.bfloat16), 'replica', axis=1, til...  15.7 us
    psum x1, blocking collectives, body(): whole_norm = lax.psum(partial_norm[0].astype(jnp.float32), 'replica')  14 us
    reduce_scatter x1, waiting for transfers between devices, body(): lax.psum_scatter(partial_value[0].astype(jnp.float32), 'replica', scatter...  12.1 us
    reduce_scatter x1, waiting for transfers between devices, body(): lax.psum_scatter(partial_mixed[0].astype(jnp.float32), 'replica', scatter...  11.8 us
    reduce_scatter x1, waiting for transfers between devices, body(): lax.psum_scatter(partial_key[0].astype(jnp.float32), 'replica', scatter_d...  10.9 us
  transfers between devices with their start and end apart: 4, of which 4 were waited for; matrix products, arithmetic and copies ran while one was open for 6% of the time, Pallas kernels for 0%

commit v1 on v0

--- a/solution.py
+++ b/solution.py
@@ -5,9 +5,86 @@
 
 learn_rate = 0.05
 hold_rate = 0.7
-
-
-def body(
+GROUPS = ((0, 1), (2, 3))
+
+
+def cut(x, place, parts, axis):
+    size = x.shape[axis] // parts
+    return lax.dynamic_slice_in_dim(x, place * size, size, axis)
+
+
+def update(mean, master, memory):
+    state = hold_rate * memory + (1.0 - hold_rate) * mean * mean
+    return master - learn_rate * mean * lax.rsqrt(state + 1e-06), state
+
+
+def shift(x, step, parts):
+    return lax.ppermute(x, "replica", [(k, (k + step) % parts) for k in range(parts)])
+
+
+def place_pieces(pieces, me, axis):
+    parts = len(pieces)
+    size = pieces[0].shape[axis]
+    shape = list(pieces[0].shape)
+    shape[axis] = size * parts
+    out = jnp.zeros(shape, pieces[0].dtype)
+    for step, piece in enumerate(pieces):
+        out = lax.dynamic_update_slice_in_dim(out, piece, (me + parts - step) % parts * size, axis)
+    return out
+
+
+def gather(mine, axis_list, me, parts):
+    packed = jnp.concatenate(mine, axis=0)
+    up, down = packed, packed
+    got = {0: packed}
+    for s in range(1, parts // 2 + 1):
+        up = shift(up, 1, parts)
+        got[s] = up
+        if parts - s not in got:
+            down = shift(down, parts - 1, parts)
+            got[parts - s] = down
+    pieces = [got[s] for s in range(parts)]
+    outs, row = [], 0
+    for m, a in zip(mine, axis_list):
+        h = m.shape[0]
+        outs.append(place_pieces([p[row:row + h] for p in pieces], me, a))
+        row += h
+    return outs
+
+
+def few(*args):
+    partials, masters, memories = args[:5], args[5:10], args[10:]
+    parts = lax.axis_size("replica")
+    me = lax.axis_index("replica")
+    rate = parts ** (-0.5)
+    axes = (0, 0, 0, 1)
+    compute, stepped, state = [None] * 5, [None] * 5, [None] * 5
+    pn = partials[4][0].reshape(parts, -1)
+    norm_in = [lax.dynamic_index_in_dim(pn, (me + s) % parts, 0, keepdims=True) for s in range(parts)]
+    norm_in = [norm_in[0]] + [shift(norm_in[s], s, parts) for s in range(1, parts)]
+    mean_norm = sum(x[0].astype(jnp.float32) for x in norm_in) * rate
+    stepped[4], state[4] = update(mean_norm, masters[4], memories[4])
+    low = stepped[4].astype(jnp.bfloat16)[None]
+    npieces = [low] + [shift(low, s, parts) for s in range(1, parts)]
+    compute[4] = place_pieces(npieces, me, 0).reshape(-1)
+    for group in GROUPS:
+        got = [[cut(partials[t][0], me, parts, axes[t]).astype(jnp.float32) for t in group]]
+        for s in range(1, parts):
+            packed = jnp.concatenate([cut(partials[t][0], (me + s) % parts, parts, axes[t]) for t in group], axis=0)
+            packed = shift(packed, s, parts)
+            h = packed.shape[0] // len(group)
+            got.append([packed[k * h:(k + 1) * h].astype(jnp.float32) for k in range(len(group))])
+        sums = [sum(g[k] for g in got) for k in range(len(group))]
+        lows = []
+        for t, total in zip(group, sums):
+            stepped[t], state[t] = update(total * rate, masters[t], memories[t])
+            lows.append(stepped[t].astype(jnp.bfloat16))
+        for t, o in zip(group, gather(lows, [axes[t] for t in group], me, parts)):
+            compute[t] = o
+    return tuple(compute + stepped + state)
+
+
+def plain(
     partial_query,
     partial_key,
     partial_value,
@@ -85,6 +162,15 @@
     )
 
 
+def body(*args):
+    parts = lax.axis_size("replica")
+    tall = (args[0].shape[1] // parts, args[0].shape[2])
+    wide = (args[3].shape[1], args[3].shape[2] // parts)
+    if parts <= 4 and tall == wide:
+        return few(*args)
+    return plain(*args)
+
+
 def solution(mesh):
     placed = (
         P(("site", "replica"), None, "model"),

time: 168 us -> 98.6 us (0.59)
  blocking collectives: 96.2 us -> 0 us
  starting transfers between devices: 0.16 us -> 47.3 us
  between operations: 13.8 us -> 1.01 us
  other arithmetic: 13.3 us -> 5.67 us
    all_gather x5 -> x0, blocking collectives: 82.2 us -> none  [the longest x1 19.7 us: body(): lax.all_gather(stepped_key.astype(jnp.bfloat16), 'replica', axis=0, tiled...]
    ppermute x0 -> x18, starting transfers between devices: none -> 47.3 us  [shift(): lax.ppermute(x, 'replica', [(k, (k + step) % parts) for k in range(parts)])]
    ppermute x0 -> x18, waiting for transfers between devices: none -> 37.6 us  [shift(): lax.ppermute(x, 'replica', [(k, (k + step) % parts) for k in range(parts)])]
    reduce_scatter x4 -> x0, waiting for transfers between devices: 36.1 us -> none  [the longest x1 12.1 us: body(): lax.psum_scatter(partial_value[0].astype(jnp.float32), 'replica', scatter...]
    psum x1 -> x0, blocking collectives: 14 us -> none  [body(): whole_norm = lax.psum(partial_norm[0].astype(jnp.float32), 'replica')]
    convert_element_type x10 -> x1, other arithmetic: 13.3 us -> 0.57 us  [few(): low = stepped[4].astype(jnp.bfloat16)[None]]
    dynamic_update_slice x0 -> x3, other arithmetic: none -> 4.21 us  [place_pieces(): lax.dynamic_update_slice_in_dim(out, piece, (me + parts - step) % parts *...]
    unnamed x34 -> x35, local copies, waits for them, and re-layouts: 7.35 us -> 4.98 us
  transfers between devices with their start and end apart: 4 -> 18, of which waited for: 4 -> 6; matrix products, arithmetic and copies ran while one was open for 6% -> 8% of each run, Pallas kernels for 0% -> 0%
where the time goes in v1:
time: 98.6 us; the launch traced here: 98.4 us
  starting transfers between devices  47.3 us (48%)
  waiting for transfers between devices  37.6 us (38%)
  local copies, waits for them, and re-layouts  6.77 us (7%)
  other arithmetic  5.67 us (6%)
  between operations  1.01 us (1%)
    ppermute x18, starting transfers between devices, shift(): lax.ppermute(x, 'replica', [(k, (k + step) % parts) for k in range(parts)])  47.3 us
    ppermute x18, waiting for transfers between devices, shift(): lax.ppermute(x, 'replica', [(k, (k + step) % parts) for k in range(parts)])  37.6 us
    unnamed x35, local copies, waits for them, and re-layouts  4.98 us
    dynamic_update_slice x3, other arithmetic, place_pieces(): lax.dynamic_update_slice_in_dim(out, piece, (me + parts - step) % parts *...  4.21 us
  transfers between devices with their start and end apart: 18, of which 6 were waited for; matrix products, arithmetic and copies ran while one was open for 8% of the time, Pallas kernels for 0%

profile of v1, /device:TPU:0, one launch (start us, length us, event | category | flops | bytes accessed | tf_op | source)
XLA Modules:
  0.0 98.4 jit_solution(7931828057252230009)
XLA Ops:
  0.7 0.7 copy-done.14
  1.4 3.1 %collective-permute-start.12 = (bf16[1,256]{1,0:T(2,128)(2,1)S(1)}, bf16[1,256]{1,0:T(2,128)(2,1)S(1)}, u32[]{:S(2)}, u32[]{:S(2)}) collective-permute-start(bf16[1,256]{1,0:T(2,128)(2,1)S(1)} %get-tuple-element.64), channel_id=1, source_target_pairs={{0,4},{4,8},{8,12},{12,0},{1,5},{5,9},{9,13},{13,1},{2,6},{6,10},{... | collective-permute-start | bytes 1544 | tf_op jit(solution)/shard_map/ppermute | solution.py:22
  4.5 2.6 %collective-permute-start.13 = (bf16[1,256]{1,0:T(2,128)(2,1)S(1)}, bf16[1,256]{1,0:T(2,128)(2,1)S(1)}, u32[]{:S(2)}, u32[]{:S(2)}) collective-permute-start(bf16[1,256]{1,0:T(2,128)(2,1)S(1)} %get-tuple-element.66), channel_id=1, source_target_pairs={{0,8},{4,12},{8,0},{12,4},{1,9},{5,13},{9,1},{13,5},{2,10},{6,14},... | collective-permute-start | bytes 1544 | tf_op jit(solution)/shard_map/ppermute | solution.py:22
  7.1 1.3 %dynamic-slice_bitcast_fusion.4 = (bf16[256,256]{1,0:T(8,128)(2,1)S(1)}, bf16[256,256]{1,0:T(8,128)(2,1)S(1)}, bf16[256,256]{1,0:T(8,128)(2,1)S(1)}, bf16[256,25...) fusion(bf16[1,256,1024]{2,1,0:T(8,128)(2,1)} %param.18, s32[]{:T(128)S(6)} %select_n.148, ...), kind=kLoop, calls=%fused_computation.44 | loop fusion | bytes 1572876 | tf_op jit(solution)/shard_map/dynamic_slice | solution.py:13
  8.4 0.1 collective-permute-start.6
  8.6 1.9 %collective-permute-start.7 = (bf16[512,256]{1,0:T(8,128)(2,1)S(1)}, bf16[512,256]{1,0:T(8,128)(2,1)}, u32[]{:S(2)}, u32[]{:S(2)}) collective-permute-start(bf16[512,256]{1,0:T(8,128)(2,1)S(1)} %pad_maximum_fusion.5), channel_id=1, source_target_pairs={{0,8},{4,12},{8,0},{12,4},{1,9},{5,13},{9,1},{13,5},{2,10},{6,14},... | collective-permute-start | bytes 786440 | tf_op jit(solution)/shard_map/ppermute | solution.py:22
  10.5 2.0 %collective-permute-start.8 = (bf16[512,256]{1,0:T(8,128)(2,1)S(1)}, bf16[512,256]{1,0:T(8,128)(2,1)}, u32[]{:S(2)}, u32[]{:S(2)}) collective-permute-start(bf16[512,256]{1,0:T(8,128)(2,1)S(1)} %pad_maximum_fusion.6), channel_id=1, source_target_pairs={{0,12},{4,0},{8,4},{12,8},{1,13},{5,1},{9,5},{13,9},{2,14},{6,2},{... | collective-permute-start | bytes 786440 | tf_op jit(solution)/shard_map/ppermute | solution.py:22
  12.5 0.0 copy-done.4
  12.5 0.1 dynamic-slice_bitcast_fusion.10
  12.7 0.0 collective-permute-done.12
  12.7 1.1 %collective-permute-start.14 = (bf16[1,256]{1,0:T(2,128)(2,1)S(1)}, bf16[1,256]{1,0:T(2,128)(2,1)S(1)}, u32[]{:S(2)}, u32[]{:S(2)}) collective-permute-start(bf16[1,256]{1,0:T(2,128)(2,1)S(1)} %get-tuple-element.65), channel_id=1, source_target_pairs={{0,12},{4,0},{8,4},{12,8},{1,13},{5,1},{9,5},{13,9},{2,14},{6,2},{... | collective-permute-start | bytes 1544 | tf_op jit(solution)/shard_map/ppermute | solution.py:22
  13.7 0.0 collective-permute-done.13
  13.7 1.0 %collective-permute-start = (bf16[512,256]{1,0:T(8,128)(2,1)S(1)}, bf16[512,256]{1,0:T(8,128)(2,1)S(1)}, u32[]{:S(2)}, u32[]{:S(2)}) collective-permute-start(bf16[512,256]{1,0:T(8,128)(2,1)S(1)} %pad_maximum_fusion), channel_id=1, source_target_pairs={{0,4},{4,8},{8,12},{12,0},{1,5},{5,9},{9,13},{13,1},{2,6},{6,10},{... | collective-permute-start | bytes 786440 | tf_op jit(solution)/shard_map/ppermute | solution.py:22
  14.7 11.9 %collective-permute-done.14 = bf16[1,256]{1,0:T(2,128)(2,1)S(1)} collective-permute-done((bf16[1,256]{1,0:T(2,128)(2,1)S(1)}, bf16[1,256]{1,0:T(2,128)(2,1)S(1)}, u32[]{:S(2)}, u32[]{:S(2)}) %collective-permute-start.14) | collective-permute-done | bytes 544 | tf_op jit(solution)/shard_map/ppermute | solution.py:22
  26.6 12.8 %collective-permute-start.1 = (bf16[512,256]{1,0:T(8,128)(2,1)S(1)}, bf16[512,256]{1,0:T(8,128)(2,1)S(1)}, u32[]{:S(2)}, u32[]{:S(2)}) collective-permute-start(bf16[512,256]{1,0:T(8,128)(2,1)S(1)} %pad_maximum_fusion.1), channel_id=1, source_target_pairs={{0,8},{4,12},{8,0},{12,4},{1,9},{5,13},{9,1},{13,5},{2,10},{6,14},... | collective-permute-start | bytes 786440 | tf_op jit(solution)/shard_map/ppermute | solution.py:22
  39.4 0.0 collective-permute-done.6
  39.4 3.5 %collective-permute-start.2 = (bf16[512,256]{1,0:T(8,128)(2,1)S(1)}, bf16[512,256]{1,0:T(8,128)(2,1)S(1)}, u32[]{:S(2)}, u32[]{:S(2)}) collective-permute-start(bf16[512,256]{1,0:T(8,128)(2,1)S(1)} %pad_maximum_fusion.2), channel_id=1, source_target_pairs={{0,12},{4,0},{8,4},{12,8},{1,13},{5,1},{9,5},{13,9},{2,14},{6,2},{... | collective-permute-start | bytes 786440 | tf_op jit(solution)/shard_map/ppermute | solution.py:22
  43.0 0.0 collective-permute-done.7
  43.0 0.0 collective-permute-done.8
  43.0 0.0 copy-start.13
  43.0 0.0 copy-start.10
  43.0 0.0 copy-start.11
  43.1 0.1 broadcast_in_dim.9
  43.1 0.8 copy-done.12
  43.9 0.1 copy-done.13
  44.0 0.1 copy-done.10
  44.1 0.1 copy-done.11
  44.2 2.3 %constant_dynamic-update-slice_fusion = (bf16[256,1024]{1,0:T(8,128)(2,1)S(1)}, bf16[256,256]{1,0:T(8,128)(2,1)S(1)}, f32[256,256]{1,0:T(8,128)}, f32[256,256]{1...) fusion(bf16[256,1024]{1,0:T(8,128)(2,1)S(1)} %broadcast_in_dim., ...), kind=kLoop, calls=%fused_computation.56 | loop fusion | flops 2228224 | bytes 3670024 | tf_op jit(solution)/shard_map/dynamic_update_slice | solution.py:32
  46.5 0.7 pad_maximum_fusion.7
  47.2 0.0 collective-permute-start.9
  47.2 0.0 collective-permute-done
  47.2 5.4 %collective-permute-done.1 = bf16[512,256]{1,0:T(8,128)(2,1)S(1)} collective-permute-done((bf16[512,256]{1,0:T(8,128)(2,1)S(1)}, bf16[512,256]{1,0:T(8,128)(2,1)S(1)}, u32[]{:S(2)}, u32[]{:S(2)}) %collective-permute-start.1) | collective-permute-done | bytes 262176 | tf_op jit(solution)/shard_map/ppermute | solution.py:22
  52.6 0.0 collective-permute-done.2
  52.7 0.9 constant_dynamic-update-slice_fusion.3
  53.7 0.9 copy-done.8
  54.6 0.1 copy-done.9
  54.7 0.9 constant_dynamic-update-slice_fusion.2
  55.6 10.0 %collective-permute-start.3 = (bf16[512,256]{1,0:T(8,128)(2,1)S(1)}, bf16[512,256]{1,0:T(8,128)(2,1)S(1)}, u32[]{:S(2)}, u32[]{:S(2)}) collective-permute-start(bf16[512,256]{1,0:T(8,128)(2,1)S(1)} %pad_maximum_fusion.3), channel_id=1, source_target_pairs={{0,4},{4,8},{8,12},{12,0},{1,5},{5,9},{9,13},{13,1},{2,6},{6,10},{... | collective-permute-start | bytes 786440 | tf_op jit(solution)/shard_map/ppermute | solution.py:22
  65.7 0.7 copy-done.15
  66.4 0.6 fusion.12
  66.9 0.0 collective-permute-start.15
  67.0 0.0 collective-permute-start.16
  67.0 3.8 %collective-permute-start.17 = (bf16[1,256]{1,0:T(2,128)(2,1)S(1)}, bf16[1,256]{1,0:T(2,128)(2,1)S(1)}, u32[]{:S(2)}, u32[]{:S(2)}) collective-permute-start(bf16[1,256]{1,0:T(2,128)(2,1)S(1)} %broadcast_in_dim.11), channel_id=1, source_target_pairs={{0,12},{4,0},{8,4},{12,8},{1,13},{5,1},{9,5},{13,9},{2,14},{6,2},{... | collective-permute-start | bytes 1544 | tf_op jit(solution)/shard_map/ppermute | solution.py:22
  70.8 1.5 %collective-permute-done.15 = bf16[1,256]{1,0:T(2,128)(2,1)S(1)} collective-permute-done((bf16[1,256]{1,0:T(2,128)(2,1)S(1)}, bf16[1,256]{1,0:T(2,128)(2,1)S(1)}, u32[]{:S(2)}, u32[]{:S(2)}) %collective-permute-start.15) | collective-permute-done | bytes 544 | tf_op jit(solution)/shard_map/ppermute | solution.py:22
  72.3 0.0 collective-permute-done.16
  72.4 0.5 collective-permute-done.17
  72.9 0.6 copy.30
  73.5 3.3 %collective-permute-start.11 = (bf16[512,256]{1,0:T(8,128)(2,1)}, bf16[512,256]{1,0:T(8,128)(2,1)S(1)}, u32[]{:S(2)}, u32[]{:S(2)}) collective-permute-start(bf16[512,256]{1,0:T(8,128)(2,1)} %pad_maximum_fusion.7), channel_id=1, source_target_pairs={{0,12},{4,0},{8,4},{12,8},{1,13},{5,1},{9,5},{13,9},{2,14},{6,2},{... | collective-permute-start | bytes 786440 | tf_op jit(solution)/shard_map/ppermute | solution.py:22
  76.8 0.0 collective-permute-start.5
  76.8 0.0 collective-permute-done.9
  76.8 2.0 %collective-permute-start.10 = (bf16[512,256]{1,0:T(8,128)(2,1)S(1)}, bf16[512,256]{1,0:T(8,128)(2,1)S(1)}, u32[]{:S(2)}, u32[]{:S(2)}) collective-permute-start(bf16[512,256]{1,0:T(8,128)(2,1)S(1)} %collective-permute-done.9), channel_id=1, source_target_pairs={{0,4},{4,8},{8,12},{12,0},{1,5},{5,9},{9,13},{13,1},{2,6},{6,10},{... | collective-permute-start | bytes 786440 | tf_op jit(solution)/shard_map/ppermute | solution.py:22
  78.8 0.0 collective-permute-done.3
  78.8 0.1 collective-permute-start.4
  78.9 15.6 %collective-permute-done.10 = bf16[512,256]{1,0:T(8,128)(2,1)S(1)} collective-permute-done((bf16[512,256]{1,0:T(8,128)(2,1)S(1)}, bf16[512,256]{1,0:T(8,128)(2,1)S(1)}, u32[]{:S(2)}, u32[]{:S(2)}) %collective-permute-start.10) | collective-permute-done | bytes 262176 | tf_op jit(solution)/shard_map/ppermute | solution.py:22
  94.5 0.0 collective-permute-done.11
  94.6 0.0 copy-start
  94.6 0.0 copy-start.1
  94.6 2.7 %collective-permute-done.4 = bf16[512,256]{1,0:T(8,128)(2,1)S(1)} collective-permute-done((bf16[512,256]{1,0:T(8,128)(2,1)S(1)}, bf16[512,256]{1,0:T(8,128)(2,1)S(1)}, u32[]{:S(2)}, u32[]{:S(2)}) %collective-permute-start.4) | collective-permute-done | bytes 262176 | tf_op jit(solution)/shard_map/ppermute | solution.py:22
  97.3 0.0 collective-permute-done.5
  97.4 0.0 copy-done
  97.4 0.0 copy-start.2
  97.4 0.0 copy-start.3
  97.4 0.8 copy-done.2
  98.2 0.2 copy-done.3
  (42 shorter events, 0.6 us)
Async XLA Ops:
  0.7 0.7 copy-start.14
  1.4 11.2 %collective-permute-start.12 = (bf16[1,256]{1,0:T(2,128)(2,1)S(1)}, bf16[1,256]{1,0:T(2,128)(2,1)S(1)}, u32[]{:S(2)}, u32[]{:S(2)}) collective-permute-start(bf16[1,256]{1,0:T(2,128)(2,1)S(1)} %get-tuple-element.64), channel_id=1, source_target_pairs={{0,4},{4,8},{8,12},{12,0},{1,5},{5,9},{9,13},{13,1},{2,6},{6,10},{... | collective-permute-start | bytes 1544 | tf_op jit(solution)/shard_map/ppermute | solution.py:22
  4.5 9.2 %collective-permute-start.13 = (bf16[1,256]{1,0:T(2,128)(2,1)S(1)}, bf16[1,256]{1,0:T(2,128)(2,1)S(1)}, u32[]{:S(2)}, u32[]{:S(2)}) collective-permute-start(bf16[1,256]{1,0:T(2,128)(2,1)S(1)} %get-tuple-element.66), channel_id=1, source_target_pairs={{0,8},{4,12},{8,0},{12,4},{1,9},{5,13},{9,1},{13,5},{2,10},{6,14},... | collective-permute-start | bytes 1544 | tf_op jit(solution)/shard_map/ppermute | solution.py:22
  8.4 31.0 %collective-permute-start.6 = (bf16[512,256]{1,0:T(8,128)(2,1)S(1)}, bf16[512,256]{1,0:T(8,128)(2,1)S(1)}, u32[]{:S(2)}, u32[]{:S(2)}) collective-permute-start(bf16[512,256]{1,0:T(8,128)(2,1)S(1)} %pad_maximum_fusion.4), channel_id=1, source_target_pairs={{0,4},{4,8},{8,12},{12,0},{1,5},{5,9},{9,13},{13,1},{2,6},{6,10},{... | collective-permute-start | bytes 786440 | tf_op jit(solution)/shard_map/ppermute | solution.py:22
  8.6 3.9 %copy-start.4 = (bf16[1,1024,256]{2,1,0:T(8,128)(2,1)S(1)}, bf16[1,1024,256]{2,1,0:T(8,128)(2,1)}, u32[]{:S(2)}) copy-start(bf16[1,1024,256]{2,1,0:T(8,128)(2,1)} %param.15) | copy-start | bytes 1572868
  8.6 3.9 %copy-start.5 = (bf16[1,1024,256]{2,1,0:T(8,128)(2,1)S(1)}, bf16[1,1024,256]{2,1,0:T(8,128)(2,1)}, u32[]{:S(2)}) copy-start(bf16[1,1024,256]{2,1,0:T(8,128)(2,1)} %param.16) | copy-start | bytes 1572868
  8.6 34.4 %collective-permute-start.7 = (bf16[512,256]{1,0:T(8,128)(2,1)S(1)}, bf16[512,256]{1,0:T(8,128)(2,1)}, u32[]{:S(2)}, u32[]{:S(2)}) collective-permute-start(bf16[512,256]{1,0:T(8,128)(2,1)S(1)} %pad_maximum_fusion.5), channel_id=1, source_target_pairs={{0,8},{4,12},{8,0},{12,4},{1,9},{5,13},{9,1},{13,5},{2,10},{6,14},... | collective-permute-start | bytes 786440 | tf_op jit(solution)/shard_map/ppermute | solution.py:22
  10.5 32.5 %collective-permute-start.8 = (bf16[512,256]{1,0:T(8,128)(2,1)S(1)}, bf16[512,256]{1,0:T(8,128)(2,1)}, u32[]{:S(2)}, u32[]{:S(2)}) collective-permute-start(bf16[512,256]{1,0:T(8,128)(2,1)S(1)} %pad_maximum_fusion.6), channel_id=1, source_target_pairs={{0,12},{4,0},{8,4},{12,8},{1,13},{5,1},{9,5},{13,9},{2,14},{6,2},{... | collective-permute-start | bytes 786440 | tf_op jit(solution)/shard_map/ppermute | solution.py:22
  12.7 13.9 %collective-permute-start.14 = (bf16[1,256]{1,0:T(2,128)(2,1)S(1)}, bf16[1,256]{1,0:T(2,128)(2,1)S(1)}, u32[]{:S(2)}, u32[]{:S(2)}) collective-permute-start(bf16[1,256]{1,0:T(2,128)(2,1)S(1)} %get-tuple-element.65), channel_id=1, source_target_pairs={{0,12},{4,0},{8,4},{12,8},{1,13},{5,1},{9,5},{13,9},{2,14},{6,2},{... | collective-permute-start | bytes 1544 | tf_op jit(solution)/shard_map/ppermute | solution.py:22
  13.7 33.5 %collective-permute-start = (bf16[512,256]{1,0:T(8,128)(2,1)S(1)}, bf16[512,256]{1,0:T(8,128)(2,1)S(1)}, u32[]{:S(2)}, u32[]{:S(2)}) collective-permute-start(bf16[512,256]{1,0:T(8,128)(2,1)S(1)} %pad_maximum_fusion), channel_id=1, source_target_pairs={{0,4},{4,8},{8,12},{12,0},{1,5},{5,9},{9,13},{13,1},{2,6},{6,10},{... | collective-permute-start | bytes 786440 | tf_op jit(solution)/shard_map/ppermute | solution.py:22
  26.6 26.0 %collective-permute-start.1 = (bf16[512,256]{1,0:T(8,128)(2,1)S(1)}, bf16[512,256]{1,0:T(8,128)(2,1)S(1)}, u32[]{:S(2)}, u32[]{:S(2)}) collective-permute-start(bf16[512,256]{1,0:T(8,128)(2,1)S(1)} %pad_maximum_fusion.1), channel_id=1, source_target_pairs={{0,8},{4,12},{8,0},{12,4},{1,9},{5,13},{9,1},{13,5},{2,10},{6,14},... | collective-permute-start | bytes 786440 | tf_op jit(solution)/shard_map/ppermute | solution.py:22
  39.4 13.2 %collective-permute-start.2 = (bf16[512,256]{1,0:T(8,128)(2,1)S(1)}, bf16[512,256]{1,0:T(8,128)(2,1)S(1)}, u32[]{:S(2)}, u32[]{:S(2)}) collective-permute-start(bf16[512,256]{1,0:T(8,128)(2,1)S(1)} %pad_maximum_fusion.2), channel_id=1, source_target_pairs={{0,12},{4,0},{8,4},{12,8},{1,13},{5,1},{9,5},{13,9},{2,14},{6,2},{... | collective-permute-start | bytes 786440 | tf_op jit(solution)/shard_map/ppermute | solution.py:22
  43.0 1.0 copy-start.12
  43.0 1.0 %copy-start.13 = (f32[256,256]{1,0:T(8,128)S(1)}, f32[256,256]{1,0:T(8,128)}, u32[]{:S(2)}) copy-start(f32[256,256]{1,0:T(8,128)} %param.27) | copy-start | bytes 786436
  43.0 1.1 %copy-start.10 = (f32[256,256]{1,0:T(8,128)S(1)}, f32[256,256]{1,0:T(8,128)}, u32[]{:S(2)}) copy-start(f32[256,256]{1,0:T(8,128)} %param.23) | copy-start | bytes 786436
  43.0 1.1 %copy-start.11 = (f32[256,256]{1,0:T(8,128)S(1)}, f32[256,256]{1,0:T(8,128)}, u32[]{:S(2)}) copy-start(f32[256,256]{1,0:T(8,128)} %param.28) | copy-start | bytes 786436
  47.2 5.4 %copy-start.6 = (f32[256,256]{1,0:T(8,128)S(1)}, f32[256,256]{1,0:T(8,128)}, u32[]{:S(2)}) copy-start(f32[256,256]{1,0:T(8,128)} %param.20) | copy-start | bytes 786436
  47.2 5.5 %copy-start.7 = (f32[256,256]{1,0:T(8,128)S(1)}, f32[256,256]{1,0:T(8,128)}, u32[]{:S(2)}) copy-start(f32[256,256]{1,0:T(8,128)} %param.25) | copy-start | bytes 786436
  47.2 29.6 %collective-permute-start.9 = (bf16[512,256]{1,0:T(8,128)(2,1)}, bf16[512,256]{1,0:T(8,128)(2,1)S(1)}, u32[]{:S(2)}, u32[]{:S(2)}) collective-permute-start(bf16[512,256]{1,0:T(8,128)(2,1)} %pad_maximum_fusion.7), channel_id=1, source_target_pairs={{0,4},{4,8},{8,12},{12,0},{1,5},{5,9},{9,13},{13,1},{2,6},{6,10},{... | collective-permute-start | bytes 786440 | tf_op jit(solution)/shard_map/ppermute | solution.py:22
  53.6 0.9 copy-start.8
  53.6 1.0 %copy-start.9 = (f32[256,256]{1,0:T(8,128)S(1)}, f32[256,256]{1,0:T(8,128)}, u32[]{:S(2)}) copy-start(f32[256,256]{1,0:T(8,128)} %param.26) | copy-start | bytes 786436
  55.6 10.1 %copy-start.16 = (f32[256]{0:T(256)S(1)}, f32[256]{0:T(256)}, u32[]{:S(2)}) copy-start(f32[256]{0:T(256)} %param.29) | copy-start | bytes 3076
  55.6 23.2 %collective-permute-start.3 = (bf16[512,256]{1,0:T(8,128)(2,1)S(1)}, bf16[512,256]{1,0:T(8,128)(2,1)S(1)}, u32[]{:S(2)}, u32[]{:S(2)}) collective-permute-start(bf16[512,256]{1,0:T(8,128)(2,1)S(1)} %pad_maximum_fusion.3), channel_id=1, source_target_pairs={{0,4},{4,8},{8,12},{12,0},{1,5},{5,9},{9,13},{13,1},{2,6},{6,10},{... | collective-permute-start | bytes 786440 | tf_op jit(solution)/shard_map/ppermute | solution.py:22
  65.7 0.7 copy-start.15
  66.9 5.4 %collective-permute-start.15 = (bf16[1,256]{1,0:T(2,128)(2,1)S(1)}, bf16[1,256]{1,0:T(2,128)(2,1)S(1)}, u32[]{:S(2)}, u32[]{:S(2)}) collective-permute-start(bf16[1,256]{1,0:T(2,128)(2,1)S(1)} %broadcast_in_dim.11), channel_id=1, source_target_pairs={{0,4},{4,8},{8,12},{12,0},{1,5},{5,9},{9,13},{13,1},{2,6},{6,10},{... | collective-permute-start | bytes 1544 | tf_op jit(solution)/shard_map/ppermute | solution.py:22
  67.0 5.4 %collective-permute-start.16 = (bf16[1,256]{1,0:T(2,128)(2,1)S(1)}, bf16[1,256]{1,0:T(2,128)(2,1)S(1)}, u32[]{:S(2)}, u32[]{:S(2)}) collective-permute-start(bf16[1,256]{1,0:T(2,128)(2,1)S(1)} %broadcast_in_dim.11), channel_id=1, source_target_pairs={{0,8},{4,12},{8,0},{12,4},{1,9},{5,13},{9,1},{13,5},{2,10},{6,14},... | collective-permute-start | bytes 1544 | tf_op jit(solution)/shard_map/ppermute | solution.py:22
  67.0 5.9 %collective-permute-start.17 = (bf16[1,256]{1,0:T(2,128)(2,1)S(1)}, bf16[1,256]{1,0:T(2,128)(2,1)S(1)}, u32[]{:S(2)}, u32[]{:S(2)}) collective-permute-start(bf16[1,256]{1,0:T(2,128)(2,1)S(1)} %broadcast_in_dim.11), channel_id=1, source_target_pairs={{0,12},{4,0},{8,4},{12,8},{1,13},{5,1},{9,5},{13,9},{2,14},{6,2},{... | collective-permute-start | bytes 1544 | tf_op jit(solution)/shard_map/ppermute | solution.py:22
  73.5 21.0 %collective-permute-start.11 = (bf16[512,256]{1,0:T(8,128)(2,1)}, bf16[512,256]{1,0:T(8,128)(2,1)S(1)}, u32[]{:S(2)}, u32[]{:S(2)}) collective-permute-start(bf16[512,256]{1,0:T(8,128)(2,1)} %pad_maximum_fusion.7), channel_id=1, source_target_pairs={{0,12},{4,0},{8,4},{12,8},{1,13},{5,1},{9,5},{13,9},{2,14},{6,2},{... | collective-permute-start | bytes 786440 | tf_op jit(solution)/shard_map/ppermute | solution.py:22
  76.8 20.6 %collective-permute-start.5 = (bf16[512,256]{1,0:T(8,128)(2,1)S(1)}, bf16[512,256]{1,0:T(8,128)(2,1)S(1)}, u32[]{:S(2)}, u32[]{:S(2)}) collective-permute-start(bf16[512,256]{1,0:T(8,128)(2,1)S(1)} %pad_maximum_fusion.3), channel_id=1, source_target_pairs={{0,12},{4,0},{8,4},{12,8},{1,13},{5,1},{9,5},{13,9},{2,14},{6,2},{... | collective-permute-start | bytes 786440 | tf_op jit(solution)/shard_map/ppermute | solution.py:22
  76.8 17.7 %collective-permute-start.10 = (bf16[512,256]{1,0:T(8,128)(2,1)S(1)}, bf16[512,256]{1,0:T(8,128)(2,1)S(1)}, u32[]{:S(2)}, u32[]{:S(2)}) collective-permute-start(bf16[512,256]{1,0:T(8,128)(2,1)S(1)} %collective-permute-done.9), channel_id=1, source_target_pairs={{0,4},{4,8},{8,12},{12,0},{1,5},{5,9},{9,13},{13,1},{2,6},{6,10},{... | collective-permute-start | bytes 786440 | tf_op jit(solution)/shard_map/ppermute | solution.py:22
  78.8 18.5 %collective-permute-start.4 = (bf16[512,256]{1,0:T(8,128)(2,1)S(1)}, bf16[512,256]{1,0:T(8,128)(2,1)S(1)}, u32[]{:S(2)}, u32[]{:S(2)}) collective-permute-start(bf16[512,256]{1,0:T(8,128)(2,1)S(1)} %collective-permute-done.3), channel_id=1, source_target_pairs={{0,4},{4,8},{8,12},{12,0},{1,5},{5,9},{9,13},{13,1},{2,6},{6,10},{... | collective-permute-start | bytes 786440 | tf_op jit(solution)/shard_map/ppermute | solution.py:22
  94.6 2.8 %copy-start = (bf16[1024,256]{1,0:T(8,128)(2,1)}, bf16[1024,256]{1,0:T(8,128)(2,1)S(1)}, u32[]{:S(2)}) copy-start(bf16[1024,256]{1,0:T(8,128)(2,1)S(1)} %get-tuple-element.53) | copy-start | bytes 1572868
  94.6 2.8 %copy-start.1 = (bf16[256,1024]{1,0:T(8,128)(2,1)}, bf16[256,1024]{1,0:T(8,128)(2,1)S(1)}, u32[]{:S(2)}) copy-start(bf16[256,1024]{1,0:T(8,128)(2,1)S(1)} %get-tuple-element.52) | copy-start | bytes 1572868
  97.4 0.8 copy-start.2
  97.4 1.0 copy-start.3
